TPU v7x, 128 devices: a whole 4x4x4 slice. The times are simulated.
128 devices in a mesh: row: 8 (over z, core), col: 16 (over x, y).
Axes of the slice: x: 4, y: 4, z: 4, core: 2. Of those that a mesh axis runs over, the one named last changes fastest.
Arguments:
- activations: bfloat16 [8192, 8192], P('row', 'col'), may hold values from -6 to 6
- errors: bfloat16 [8192, 8192], P('row', 'col'), may hold values from -6 to 6
- act_proj: bfloat16 [8192, 128], P('col'), may hold values from -0.0625 to 0.0625
- err_proj: bfloat16 [8192, 128], P('col'), may hold values from -0.0625 to 0.0625
- lengths: int32 [8, 64], P('row'), may hold values from 1 to 256, 1024 in all within a row
- ridge: float32 [16384, 16384], P('row', 'col'), may hold values from -4 to 36, as said below
- pivot_inverse: float32 [2, 512, 512], replicated, may hold values from -1 to 1
Outputs:
- eliminated: float32 [16384, 16384], P('row', 'col')
Inputs may be any that keep to these rules, and one draw needn't show every extreme that they name: The lengths of one row group sum to 1024. `ridge`: Symmetric.
All inputs are finite; a program needn't handle non-finite values.
Results may differ from a plain program's by a relative error of at most 0.0074.
Values may be sent and summed in bfloat16 or wider, within the bound.
A program may use at most 128 MiB of HBM per device.

v0:
```python
import jax
import jax.numpy as jnp
from jax import lax
from jax.sharding import PartitionSpec as P


def together(arrays, axis):
    ends = [0]
    for a in arrays:
        ends.append(ends[-1] + a.size)
    running = lax.psum(jnp.concatenate([a.ravel() for a in arrays]), axis)
    return tuple((running[b:e].reshape(a.shape) for a, b, e in zip(arrays, ends, ends[1:])))


def joined_along(tiles, dim):
    tiles = jnp.moveaxis(tiles, 0, dim)
    lengths = tiles.shape
    return tiles.reshape(*lengths[:dim], lengths[dim] * lengths[dim + 1], *lengths[dim + 2 :])


def from_everyone(array, axis):
    copies = jnp.broadcast_to(array, (lax.axis_size(axis), *array.shape))
    return lax.all_to_all(copies, axis, split_axis=0, concat_axis=0, tiled=True)


def gathered_copies(array, axis, dim):
    return joined_along(from_everyone(array, axis), dim)


def spread_2(array, axis, root):
    mine = lax.axis_index(axis) == root
    return lax.psum(jnp.where(mine, array, jnp.zeros_like(array)), axis)


def as_sent(array):

    def short(part):
        return part.astype(jnp.bfloat16) if part.dtype == jnp.float32 else part

    return jax.tree.map(short, array)


def from_root(array, axis, root):
    return lax.dynamic_index_in_dim(lax.all_gather(array, axis), root, 0, keepdims=False)


def per_device(activations, errors, act_proj, err_proj, lengths, ridge, pivot_inverse):
    part_act = jnp.dot(activations, act_proj, preferred_element_type=jnp.float32)
    part_err = jnp.dot(errors, err_proj, preferred_element_type=jnp.float32)
    summed_act, summed_err = together((part_act, part_err), "col")
    proj_act = summed_act.astype(jnp.bfloat16)
    col_count = lax.axis_size("col")
    row_count = lax.axis_size("row")
    col_ratio = col_count // row_count
    col_idx = lax.axis_index("col")
    row_idx = lax.axis_index("row")
    proj_width = act_proj.shape[1]
    err_share = proj_width // col_count
    err_part = lax.dynamic_slice_in_dim(summed_err, col_idx * err_share, err_share, 1).astype(
        jnp.bfloat16
    )
    lengths_row = lengths[0]
    captions_dev = lengths_row.shape[0]
    tokens_dev = activations.shape[0]
    caption_end = jnp.cumsum(lengths_row)
    caption_start = caption_end - lengths_row
    positions = jnp.arange(tokens_dev, dtype=jnp.int32)[:, None]
    member = ((positions >= caption_start[None, :]) & (positions < caption_end[None, :])).astype(
        jnp.bfloat16
    )
    weighted = (member[:, :, None] * err_part[:, None, :]).reshape(
        tokens_dev, captions_dev * err_share
    )
    local_grads = lax.dot_general(
        weighted, proj_act, (((0,), (0,)), ((), ())), preferred_element_type=jnp.float32
    )
    local_grads = local_grads.reshape(captions_dev, err_share * proj_width).astype(jnp.bfloat16)
    col_grads = gathered_copies(local_grads, "row", 0)
    row_parts = []
    for column_step in range(col_ratio):
        row_parts.append(spread_2(col_grads, "col", row_idx * col_ratio + column_step))
    row_grads = jnp.concatenate(row_parts, axis=1)
    captions_all = col_grads.shape[0]
    gram_tile = lax.dot_general(
        row_grads, col_grads, (((0,), (0,)), ((), ())), preferred_element_type=jnp.float32
    )
    matrix = ridge + gram_tile / captions_all
    tile_rows, tile_cols = ridge.shape
    row_start = row_idx * tile_rows
    col_start = col_idx * tile_cols
    row_ids = row_start + jnp.arange(tile_rows, dtype=jnp.int32)
    col_ids = col_start + jnp.arange(tile_cols, dtype=jnp.int32)
    panel_width = pivot_inverse.shape[1]

    def apply_inverse(columns, start_col, inverse):
        result = jnp.dot(columns, inverse.T, precision=lax.Precision.HIGHEST)
        return jnp.where(row_ids[:, None] >= start_col, result, 0.0)

    first_panel = apply_inverse(matrix[:, 0:panel_width], 0, pivot_inverse[0])
    pivot_block = from_root(
        first_panel[panel_width : 2 * panel_width].astype(jnp.bfloat16), "row", 0
    ).astype(jnp.float32)
    lower_first = jnp.where(row_ids[:, None] >= panel_width, first_panel, 0.0)
    second_block = matrix[:, panel_width : 2 * panel_width] - jnp.dot(
        lower_first, pivot_block.T, precision=lax.Precision.HIGHEST
    )
    second_panel = apply_inverse(second_block, panel_width, pivot_inverse[1])
    both_panels = jnp.concatenate([first_panel, second_panel], axis=1)
    row_panel = spread_2(as_sent(both_panels), "col", 0).astype(both_panels.dtype)
    col_piece = lax.dynamic_slice_in_dim(row_panel, col_idx % col_ratio * tile_cols, tile_cols, 0)
    col_panel = spread_2(as_sent(col_piece), "row", col_idx // col_ratio).astype(col_piece.dtype)
    row_panel, col_panel = (row_panel, col_panel)
    current = matrix
    stop_col = 2 * panel_width
    lower_part = jnp.where(row_ids[:, None] >= stop_col, row_panel, 0.0)
    upper_part = jnp.where(col_ids[:, None] >= stop_col, col_panel, 0.0)
    current = current - jnp.dot(lower_part, upper_part.T, precision=lax.Precision.HIGHEST)
    offset = jnp.clip(0 - col_start, 0, tile_cols - (stop_col - 0))
    placed = lax.dynamic_update_slice(jnp.zeros_like(current), row_panel, (jnp.int32(0), offset))
    in_panel = (col_ids >= 0) & (col_ids < stop_col)
    current = jnp.where(in_panel[None, :], placed, current)
    above_panel = ((row_ids >= 0) & (row_ids < stop_col))[:, None] & (col_ids >= stop_col)[None, :]
    return jnp.where(above_panel, 0.0, current)


def solution(mesh):
    in_specs = (
        P("row", "col"),
        P("row", "col"),
        P("col", None),
        P("col", None),
        P("row", None),
        P("row", "col"),
        P(),
    )
    out_specs = P("row", "col")
    return jax.shard_map(
        per_device, mesh=mesh, in_specs=in_specs, out_specs=out_specs, check_vma=False
    )
```

profile of v0, /device:TPU:0, one launch (start us, length us, event | category | flops | bytes accessed | tf_op | source)
XLA Modules:
  0.0 489.5 jit_solution(14978960739428227277)
XLA Ops:
  6.5 0.0 copy-start
  6.5 1.2 copy-done
  7.8 0.0 copy-start.5
  7.8 1.3 convolution_bitcast_fusion
  9.1 1.7 convolution_bitcast_fusion.1
  10.8 0.1 pad_maximum_fusion
  10.8 87.9 %all-reduce.11 = bf16[262144]{0:T(1024)(128)(2,1)S(1)} all-reduce(f32[262144]{0:T(1024)S(1)} %pad_maximum_fusion), channel_id=1, replica_groups=mesh['row'=8,'col'=16] {'col'}, use_global_device_ids=true, to_apply=%region_1.0 | all-reduce | flops 262144 | bytes 1572864 | tf_op jit(solution)/shard_map/psum | solution.py:11
  98.8 0.1 constant_dynamic-slice_fusion
  98.9 0.1 copy.24
  99.0 0.0 copy-done.5
  99.1 0.1 copy.18
  99.1 0.1 reduce-window.4
  99.2 0.1 reduce
  99.4 0.1 fusion.36
  99.5 0.4 convolution_convert_fusion
  99.9 0.1 convert_element_type.36
  100.0 1.1 broadcast_in_dim.82
  101.1 5.2 %all-to-all-start = ((bf16[8,64,1024]{2,1,0:T(8,128)(2,1)}), bf16[8,64,1024]{2,1,0:T(8,128)(2,1)S(1)}, u32[]{:S(2)}, u32[]{:S(2)}) async-start(bf16[8,64,1024]{2,1,0:T(8,128)(2,1)} %broadcast_in_dim.82), calls=%async_computation | async-start | bytes 2097152 | tf_op jit(solution)/shard_map/all_to_all | solution.py:23
  106.3 0.0 all-reduce.10.cloned.1.call-start
  106.4 15.9 %all-to-all-done = bf16[8,64,1024]{2,1,0:T(8,128)(2,1)S(1)} async-done(((bf16[8,64,1024]{2,1,0:T(8,128)(2,1)}), bf16[8,64,1024]{2,1,0:T(8,128)(2,1)S(1)}, u32[]{:S(2)}, u32[]{:S(2)}) %all-to-all-start) | async-done | bytes 1048608 | tf_op jit(solution)/shard_map/all_to_all | solution.py:23
  122.3 1.5 broadcast_select_fusion.1
  123.8 0.0 all-reduce.10.cloned.1.call-update
  123.8 0.0 all-gather.3.cloned.1.call-start
  123.9 86.4 %all-reduce.10.cloned.1.call-done = (bf16[512,1024]{1,0:T(8,128)(2,1)}, bf16[512,1024]{1,0:T(8,128)(2,1)}) async-done(((bf16[512,1024]{1,0:T(8,128)(2,1)}, bf16[512,1024]{1,0:T(8,128)(2,1)}), (bf16[512,1024]{1,0:T(8,128)(2,1)}, bf16[512,1024]{1,0:T(8,128)(2,1)})) %all-reduce.10.cloned.1.call-update) | async-done | bytes 2097168 | tf_op jit(solution)/shard_map/psum | solution.py:32
  210.3 0.0 copy-start.4
  210.3 6.7 %multiply_add_fusion = f32[2048,1024]{1,0:T(8,128)S(1)} fusion(f32[2048,1024]{1,0:T(8,128)} %param.12, bf16[512,1024]{1,0:T(8,128)(2,1)S(1)} %bitcast.35, bf16[512,1024]{1,0:T(8,128)(2,1)} %get-tuple-element.5, bf16[512,1024]{1,0:T(8,128)(2,1)} %get-tuple-element.6), kind=kOutput, calls=%fused_computation.5 | convolution fusion | flops 2155872256 | bytes 19922944 | tf_op jit(solution)/shard_map/dot_general | solution.py:84
  217.0 0.0 copy-done.4
  217.0 0.0 copy-start.2
  217.0 8.3 %select_convert_fusion.1 = (bf16[2048,512]{1,0:T(8,128)(2,1)S(1)}, f32[2048,512]{1,0:T(8,128)}) fusion(pred[2048]{0:T(1024)(128)(4,1)S(1)} %fusion.40, f32[2,512,512]{2,1,0:T(8,128)S(1)} %copy-done.4, f32[2048,1024]{1,0:T(8,128)S(1)} %multiply_add_fusion), kind=kOutput, calls=%fused_computation.20 | convolution fusion | flops 6443499520 | bytes 11536384 | tf_op jit(solution)/shard_map/dot_general | solution.py:96
  225.3 0.0 copy-done.2
  225.3 0.9 slice.55
  226.2 0.0 all-gather.3.cloned.1.call-update
  226.2 0.2 all-reduce.6.cloned.1.call-start
  226.5 31.7 %all-gather.3.cloned.1.call-done = bf16[4096,512]{1,0:T(8,128)(2,1)} async-done(((bf16[512,512]{1,0:T(8,128)(2,1)}), bf16[4096,512]{1,0:T(8,128)(2,1)}) %all-gather.3.cloned.1.call-update) | async-done | bytes 4194320 | tf_op jit(solution)/shard_map/all_gather | solution.py:44
  258.2 0.0 copy-start.3
  258.2 5.7 %fusion.9 = f32[2048,512]{1,0:T(8,128)S(1)} fusion(f32[2048,512]{1,0:T(8,128)} %get-tuple-element.10, pred[2048]{0:T(1024)(128)(4,1)S(1)} %fusion.38, pred[2048]{0:T(1024)(128)(4,1)S(1)} %fusion.40, bf16[4096,512]{1,0:T(8,128)(2,1)} %all-gather.3.cloned.1.call-done), kind=kOutput, calls=%fused_computation.15 | convolution fusion | flops 6444548096 | bytes 8916992 | tf_op jit(solution)/shard_map/dot_general | solution.py:104
  263.9 0.0 copy-done.3
  263.9 8.1 %select_convert_fusion = bf16[2048,512]{1,0:T(8,128)(2,1)S(1)} fusion(f32[2048,512]{1,0:T(8,128)S(1)} %fusion.9, f32[2048,1024]{1,0:T(8,128)S(1)} %copy-done.3, pred[2048]{0:T(1024)(128)(4,1)S(1)} %fusion.38, f32[2,512,512]{2,1,0:T(8,128)} %param.13), kind=kOutput, calls=%fused_computation.14 | convolution fusion | flops 6445596672 | bytes 11536384 | tf_op jit(solution)/shard_map/dot_general | solution.py:96
  272.0 2.5 maximum_select_fusion
  274.5 0.0 all-reduce.6.cloned.1.call-update
  274.5 0.3 all-reduce.8.cloned.1.call-start
  274.8 103.0 %all-reduce.6.cloned.1.call-done = bf16[2048,1024]{1,0:T(8,128)(2,1)} async-done(((bf16[2048,1024]{1,0:T(8,128)(2,1)}), bf16[2048,1024]{1,0:T(8,128)(2,1)}) %all-reduce.6.cloned.1.call-update) | async-done | bytes 4194320 | tf_op jit(solution)/shard_map/psum | solution.py:32
  377.7 3.5 fusion.14
  381.2 0.0 all-reduce.8.cloned.1.call-update
  381.3 65.9 %all-reduce.8.cloned.1.call-done = bf16[1024,1024]{1,0:T(8,128)(2,1)} async-done(((bf16[1024,1024]{1,0:T(8,128)(2,1)}), bf16[1024,1024]{1,0:T(8,128)(2,1)}) %all-reduce.8.cloned.1.call-update) | async-done | bytes 2097168 | tf_op jit(solution)/shard_map/psum | solution.py:32
  447.2 0.0 copy-start.1
  447.2 35.8 %select_select_fusion = f32[2048,1024]{1,0:T(8,128)} fusion(f32[2048,1024]{1,0:T(8,128)} %copy-done.2, bf16[1024,1024]{1,0:T(8,128)(2,1)} %all-reduce.8.cloned.1.call-done, pred[2048]{0:T(1024)(128)(4,1)S(1)} %get-tuple-element.11, pred[1024]{0:T(1024)(128)(4,1)S(1)} %get-tuple-element.14, pred[1024]{0:T(1024)(128)(4,1)S(1)} %get-tuple-element.13, ...), kind=kOutput, calls=%fused_computation.2 | convolution fusion | flops 25786580992 | bytes 23074816 | tf_op jit(solution)/shard_map/dot_general | solution.py:117
  482.9 0.0 copy-done.1
  (6 shorter events, 0.1 us)
Async XLA Ops:
  6.5 1.2 copy-start
  7.8 91.3 %copy-start.5 = (s32[1,64]{1,0:T(1,128)S(1)}, s32[1,64]{1,0:T(1,128)}, u32[]{:S(2)}) copy-start(s32[1,64]{1,0:T(1,128)} %param.11) | copy-start | bytes 772
  101.1 21.2 %all-to-all-start = ((bf16[8,64,1024]{2,1,0:T(8,128)(2,1)}), bf16[8,64,1024]{2,1,0:T(8,128)(2,1)S(1)}, u32[]{:S(2)}, u32[]{:S(2)}) async-start(bf16[8,64,1024]{2,1,0:T(8,128)(2,1)} %broadcast_in_dim.82), calls=%async_computation | async-start | bytes 2097152 | tf_op jit(solution)/shard_map/all_to_all | solution.py:23
  106.3 103.9 %all-reduce.10.cloned.1.call-start = ((), (), s32[]{:S(2)}) async-start(), calls=%async_computation.4 | async-start | bytes 4194304 | tf_op jit(solution)/shard_map/psum | solution.py:32
  123.8 134.3 %all-gather.3.cloned.1.call-start = ((), (), s32[]{:S(2)}) async-start(), calls=%async_computation.3 | async-start | bytes 4718592 | tf_op jit(solution)/shard_map/all_gather | solution.py:44
  210.3 6.8 %copy-start.4 = (f32[2,512,512]{2,1,0:T(8,128)S(1)}, f32[2,512,512]{2,1,0:T(8,128)}, u32[]{:S(2)}) copy-start(f32[2,512,512]{2,1,0:T(8,128)} %param.13) | copy-start | bytes 6291460
  217.0 8.3 %copy-start.2 = (f32[2048,1024]{1,0:T(8,128)}, f32[2048,1024]{1,0:T(8,128)S(1)}, u32[]{:S(2)}) copy-start(f32[2048,1024]{1,0:T(8,128)S(1)} %multiply_add_fusion) | copy-start | bytes 25165828
  226.2 151.5 %all-reduce.6.cloned.1.call-start = ((), (), s32[]{:S(2)}) async-start(), calls=%async_computation.1 | async-start | bytes 8388608 | tf_op jit(solution)/shard_map/psum | solution.py:32
  258.2 5.7 %copy-start.3 = (f32[2048,1024]{1,0:T(8,128)S(1)}, f32[2048,1024]{1,0:T(8,128)}, u32[]{:S(2)}) copy-start(f32[2048,1024]{1,0:T(8,128)} %copy-done.2) | copy-start | bytes 25165828
  274.5 172.7 %all-reduce.8.cloned.1.call-start = ((), (), s32[]{:S(2)}) async-start(), calls=%async_computation.2 | async-start | bytes 4194304 | tf_op jit(solution)/shard_map/psum | solution.py:32
  447.2 35.8 %copy-start.1 = (bf16[1024,512]{1,0:T(8,128)(2,1)S(1)}, bf16[1024,512]{1,0:T(8,128)(2,1)}, u32[]{:S(2)}) copy-start(bf16[1024,512]{1,0:T(8,128)(2,1)} %param.8) | copy-start | bytes 3145732
Sparse Core Ops, SparseCore 0:
  124.0 86.2 all-reduce.9
  226.4 31.7 all-gather.2
  274.6 103.0 all-reduce.5
  381.4 65.7 all-reduce.7
where the time goes:
time: 490 us; the launch traced here: 489 us
  waiting for transfers between devices  303 us (62%)
  blocking collectives  87.9 us (18%)
  matrix products  68 us (14%)
  between operations  13.3 us (3%)
  other arithmetic  7.93 us (2%)
  starting transfers between devices  5.8 us (1%)
    psum x3, waiting for transfers between devices, spread_2(): return lax.psum(jnp.where(mine, array, jnp.zeros_like(array)), axis)  255 us
    psum x1, blocking collectives, together(): running = lax.psum(jnp.concatenate([a.ravel() for a in arrays]), axis)  87.9 us
    dot_general x1, matrix products, per_device(): jnp.dot(lower_part, upper_part.T, precision=lax.Precision.HIGHEST)  35.8 us
    all_gather x1, waiting for transfers between devices, from_root(): lax.all_gather(array, axis)  31.7 us
    dot_general x2, matrix products, apply_inverse(): result = jnp.dot(columns, inverse.T, precision=lax.Precision.HIGHEST)  16.4 us
    all_to_all x1, waiting for transfers between devices, from_everyone(): return lax.all_to_all(copies, axis, split_axis=0, concat_axis=0, tiled=True)  15.9 us
  transfers between devices with their start and end apart: 5, of which 5 were waited for; matrix products, arithmetic and copies ran while one was open for 0% of the time, Pallas kernels for 0%

commit v1 on v0

--- a/solution.py
+++ b/solution.py
@@ -29,7 +29,7 @@
 
 def spread_2(array, axis, root):
     mine = lax.axis_index(axis) == root
-    return lax.psum(jnp.where(mine, array, jnp.zeros_like(array)), axis)
+    return jnp.sum(lax.all_gather(jnp.where(mine, array, jnp.zeros_like(array)), axis), axis=0)
 
 
 def as_sent(array):

time: 490 us -> 957 us (1.95)
  waiting for transfers between devices: 303 us -> 711 us
  other arithmetic: 7.93 us -> 59.9 us
    all_gather x0 -> x4, waiting for transfers between devices: none -> 662 us  [spread_2(): lax.all_gather(jnp.where(mine, array, jnp.zeros_like(array)), axis)]
    psum x3 -> x0, waiting for transfers between devices: 255 us -> none  [spread_2(): return lax.psum(jnp.where(mine, array, jnp.zeros_like(array)), axis)]
    reduce_sum x0 -> x4, other arithmetic: none -> 51.9 us  [spread_2(): jnp.sum(lax.all_gather(jnp.where(mine, array, jnp.zeros_like(array)), axi...]
  transfers between devices with their start and end apart: 5 -> 6, of which waited for: 5 -> 6; matrix products, arithmetic and copies ran while one was open for 0% -> 1% of each run, Pallas kernels for 0% -> 0%
where the time goes in v1:
time: 957 us; the launch traced here: 955 us
  waiting for transfers between devices  711 us (74%)
  blocking collectives  87.9 us (9%)
  matrix products  67.5 us (7%)
  other arithmetic  59.9 us (6%)
  between operations  13.4 us (1%)
  local copies, waits for them, and re-layouts  10 us (1%)
    all_gather x4, waiting for transfers between devices, spread_2(): lax.all_gather(jnp.where(mine, array, jnp.zeros_like(array)), axis)  662 us
    psum x1, blocking collectives, together(): running = lax.psum(jnp.concatenate([a.ravel() for a in arrays]), axis)  87.9 us
    reduce_sum x4, other arithmetic, spread_2(): jnp.sum(lax.all_gather(jnp.where(mine, array, jnp.zeros_like(array)), axi...  51.9 us
    dot_general x1, matrix products, per_device(): jnp.dot(lower_part, upper_part.T, precision=lax.Precision.HIGHEST)  35.2 us
    all_gather x1, waiting for transfers between devices, from_root(): lax.all_gather(array, axis)  31.9 us
  transfers between devices with their start and end apart: 6, of which 6 were waited for; matrix products, arithmetic and copies ran while one was open for 1% of the time, Pallas kernels for 0%

profile of v1, /device:TPU:0, one launch (start us, length us, event | category | flops | bytes accessed | tf_op | source)
XLA Modules:
  0.0 955.4 jit_solution(8922338752593272164)
XLA Ops:
  6.5 1.2 copy-done
  7.8 1.3 convolution_bitcast_fusion
  9.1 1.7 convolution_bitcast_fusion.1
  10.8 0.1 pad_maximum_fusion
  10.8 87.9 %all-reduce.1 = bf16[262144]{0:T(1024)(128)(2,1)S(1)} all-reduce(f32[262144]{0:T(1024)S(1)} %pad_maximum_fusion), channel_id=1, replica_groups=mesh['row'=8,'col'=16] {'col'}, use_global_device_ids=true, to_apply=%region_1.0 | all-reduce | flops 262144 | bytes 1572864 | tf_op jit(solution)/shard_map/psum | solution.py:11
  98.8 0.1 constant_dynamic-slice_fusion
  98.9 0.1 copy.23
  99.1 0.1 copy.17
  99.1 0.1 reduce-window.4
  99.2 0.1 reduce.4
  99.4 0.1 fusion.37
  99.5 0.4 convolution_convert_fusion
  99.9 0.1 convert_element_type.51
  100.0 1.1 broadcast_in_dim.82
  101.1 5.2 all-to-all-start
  106.3 0.0 all-gather.8.cloned.1.call-start
  106.4 15.9 %all-to-all-done = bf16[8,64,1024]{2,1,0:T(8,128)(2,1)S(1)} async-done(((bf16[8,64,1024]{2,1,0:T(8,128)(2,1)}), bf16[8,64,1024]{2,1,0:T(8,128)(2,1)S(1)}, u32[]{:S(2)}, u32[]{:S(2)}) %all-to-all-start) | async-done | bytes 1048608 | tf_op jit(solution)/shard_map/all_to_all | solution.py:23
  122.3 1.5 broadcast_select_fusion.1
  123.7 0.0 all-gather.8.cloned.1.call-update
  123.8 0.0 all-gather.10.cloned.1.call-start
  123.8 0.7 all-gather.10.cloned.1.call-update
  124.5 0.0 all-gather.14.cloned.1.call-start
  124.6 105.7 %all-gather.8.cloned.1.call-done = bf16[16,512,1024]{2,1,0:T(8,128)(2,1)} async-done(((bf16[1,512,1024]{2,1,0:T(8,128)(2,1)}), bf16[16,512,1024]{2,1,0:T(8,128)(2,1)}) %all-gather.8.cloned.1.call-update) | async-done | bytes 16777232 | tf_op jit(solution)/shard_map/all_gather | solution.py:32
  230.3 9.3 reduce_sum.48
  239.6 103.6 %all-gather.10.cloned.1.call-done = bf16[16,512,1024]{2,1,0:T(8,128)(2,1)} async-done(((bf16[1,512,1024]{2,1,0:T(8,128)(2,1)}), bf16[16,512,1024]{2,1,0:T(8,128)(2,1)}) %all-gather.10.cloned.1.call-update) | async-done | bytes 16777232 | tf_op jit(solution)/shard_map/all_gather | solution.py:32
  343.2 9.3 reduce_sum.49
  352.6 0.0 copy-start.3
  352.6 6.1 multiply_add_fusion
  358.7 0.0 copy-start.2
  358.7 8.5 select_convert_fusion.1
  367.2 0.9 slice.55
  368.1 0.0 all-gather.14.cloned.1.call-update
  368.1 0.2 all-gather.12.cloned.1.call-start
  368.4 31.9 %all-gather.14.cloned.1.call-done = bf16[4096,512]{0,1:T(8,128)(2,1)} async-done(((bf16[512,512]{0,1:T(8,128)(2,1)}), bf16[4096,512]{0,1:T(8,128)(2,1)}) %all-gather.14.cloned.1.call-update) | async-done | bytes 4194320 | tf_op jit(solution)/shard_map/all_gather | solution.py:44
  400.2 5.6 fusion.9
  405.8 8.7 fusion.14
  414.5 2.6 maximum_select_fusion
  417.1 6.4 copy.19
  423.5 0.0 all-gather.12.cloned.1.call-update
  423.5 0.3 all-gather.16.cloned.1.call-start
  423.8 368.1 %all-gather.12.cloned.1.call-done = bf16[16,2048,1024]{2,1,0:T(8,128)(2,1)} async-done(((bf16[1,2048,1024]{2,1,0:T(8,128)(2,1)}), bf16[16,2048,1024]{2,1,0:T(8,128)(2,1)}) %all-gather.12.cloned.1.call-update) | async-done | bytes 67108880 | tf_op jit(solution)/shard_map/all_gather | solution.py:32
  791.9 23.8 %reduce_sum.50 = bf16[2048,1024]{1,0:T(8,128)(2,1)} reduce(bf16[16,2048,1024]{2,1,0:T(8,128)(2,1)} %all-gather.12.cloned.1.call-done, bf16[]{:T(256)} %constant.70.clone.1), dimensions={0}, to_apply=%region_4.5 | reduce | flops 31457280 | bytes 71303168 | tf_op jit(solution)/shard_map/reduce_sum | solution.py:32
  815.7 3.5 fusion.15
  819.1 0.0 all-gather.16.cloned.1.call-update
  819.2 84.9 %all-gather.16.cloned.1.call-done = bf16[8192,1024]{1,0:T(8,128)(2,1)} async-done(((bf16[1024,1024]{1,0:T(8,128)(2,1)}), bf16[8192,1024]{1,0:T(8,128)(2,1)}) %all-gather.16.cloned.1.call-update) | async-done | bytes 16777232 | tf_op jit(solution)/shard_map/all_gather | solution.py:32
  904.1 9.5 reduce_sum.51
  913.6 0.0 copy-start.1
  913.6 35.2 %select_select_fusion = f32[2048,1024]{1,0:T(8,128)} fusion(f32[2048,1024]{1,0:T(8,128)} %copy-done.2, bf16[1024,1024]{1,0:T(8,128)(2,1)S(1)} %reduce_sum.51, pred[2048]{0:T(1024)(128)(4,1)S(1)} %get-tuple-element.9, pred[1024]{0:T(1024)(128)(4,1)S(1)} %get-tuple-element.12, pred[1024]{0:T(1024)(128)(4,1)S(1)} %get-tuple-element.11, ...), kind=kOutput, calls=%fused_computation.2 | convolution fusion | flops 25786580992 | bytes 23074816 | tf_op jit(solution)/shard_map/dot_general | solution.py:117
  (14 shorter events, 0.1 us)
Async XLA Ops:
  6.5 1.2 copy-start
  7.8 91.3 %copy-start.5 = (s32[1,64]{1,0:T(1,128)S(1)}, s32[1,64]{1,0:T(1,128)}, u32[]{:S(2)}) copy-start(s32[1,64]{1,0:T(1,128)} %param.11) | copy-start | bytes 772
  101.1 21.2 %all-to-all-start = ((bf16[8,64,1024]{2,1,0:T(8,128)(2,1)}), bf16[8,64,1024]{2,1,0:T(8,128)(2,1)S(1)}, u32[]{:S(2)}, u32[]{:S(2)}) async-start(bf16[8,64,1024]{2,1,0:T(8,128)(2,1)} %broadcast_in_dim.82), calls=%async_computation | async-start | bytes 2097152 | tf_op jit(solution)/shard_map/all_to_all | solution.py:23
  106.3 124.0 %all-gather.8.cloned.1.call-start = ((), (), s32[]{:S(2)}) async-start(), calls=%async_computation.1 | async-start | bytes 17825792 | tf_op jit(solution)/shard_map/all_gather | solution.py:32
  123.8 219.5 %all-gather.10.cloned.1.call-start = ((), (), s32[]{:S(2)}) async-start(), calls=%async_computation.2 | async-start | bytes 17825792 | tf_op jit(solution)/shard_map/all_gather | solution.py:32
  124.5 275.7 %all-gather.14.cloned.1.call-start = ((), (), s32[]{:S(2)}) async-start(), calls=%async_computation.4 | async-start | bytes 4718592 | tf_op jit(solution)/shard_map/all_gather | solution.py:44
  352.6 6.1 copy-start.3
  358.7 8.5 copy-start.2
  368.1 423.8 %all-gather.12.cloned.1.call-start = ((), (), s32[]{:S(2)}) async-start(), calls=%async_computation.3 | async-start | bytes 71303168 | tf_op jit(solution)/shard_map/all_gather | solution.py:32
  400.2 5.6 copy-start.4
  423.5 480.6 %all-gather.16.cloned.1.call-start = ((), (), s32[]{:S(2)}) async-start(), calls=%async_computation.5 | async-start | bytes 18874368 | tf_op jit(solution)/shard_map/all_gather | solution.py:32
  913.6 35.3 %copy-start.1 = (bf16[1024,512]{1,0:T(8,128)(2,1)S(1)}, bf16[1024,512]{1,0:T(8,128)(2,1)}, u32[]{:S(2)}) copy-start(bf16[1024,512]{1,0:T(8,128)(2,1)} %param.8) | copy-start | bytes 3145732
Sparse Core Ops, SparseCore 0:
  123.9 106.3 all-gather.7
  232.4 110.7 all-gather.9
  368.2 31.9 all-gather.13
  423.6 368.1 all-gather.11
  819.3 84.8 all-gather.15
